TPU v7x, 32 devices: a whole 2x2x4 slice. The times are simulated.
32 devices in a mesh: parts: 2 (over y), gz: 4 (over z), shot: 4 (over x, core).
Axes of the slice: x: 2, y: 2, z: 4, core: 2. Of those that a mesh axis runs over, the one named last changes fastest.
Arguments:
- wavefields: float32 [8, 2, 9, 16, 32, 128], P(('parts', 'shot'), None, None, 'gz'), parts along dimension 0, may hold values from -6 to 6
- earth_model: float32 [6, 16, 32, 128], P('parts', 'gz'), parts along dimension 0, may hold values from 0.4 to 1.6
- source_depth: int32 [8], P(('parts', 'shot')), parts along dimension 0, may hold values from 0 to 15
- source_column: int32 [8], P(('parts', 'shot')), parts along dimension 0, may hold values from 0 to 4095
- wavelet: float32 [8, 8], P(('parts', 'shot')), parts along dimension 0, may hold values from -30 to 30
- receiver_depth: int32 [8, 64], P(('parts', 'shot')), parts along dimension 0, may hold values from 0 to 15
- receiver_column: int32 [8, 64], P(('parts', 'shot')), parts along dimension 0, may hold values from 0 to 4095
- traces: float32 [8, 8, 64], P(('parts', 'shot')), parts along dimension 0, may hold values from -30 to 30
Outputs:
- images: float32 [4, 16, 32, 128], P('parts', 'gz'), parts along dimension 0
There are 2 independent parts, one for each index of `parts`. A program takes and returns all parts, laid end to end along the dimension named above; each array names one. Nothing has to cross between parts.
All inputs are finite; a program needn't handle non-finite values.
Results may differ from a plain program's by a relative error of at most 0.00002.
Values sent between devices are 32-bit elements; how exact they have to be, the bound alone decides.
A program may use at most 64 MiB of HBM per device.

v0:
```python
import jax
import jax.numpy as jnp
from jax import lax
from jax.sharding import PartitionSpec as P

time_step = 0.15


def shifted(value, axis, steps):
    count = lax.axis_size(axis)
    first, last = (max(0, -steps), min(count, count - steps))
    return lax.ppermute(value, axis, [(source, source + steps) for source in range(first, last)])


def forward_diff(array, dim_index):
    length = array.shape[dim_index]
    following = jnp.concatenate(
        [
            lax.slice_in_dim(array, 1, length, axis=dim_index),
            jnp.zeros_like(lax.slice_in_dim(array, 0, 1, axis=dim_index)),
        ],
        axis=dim_index,
    )
    return following - array


def backward_diff(array, dim_index):
    length = array.shape[dim_index]
    previous = jnp.concatenate(
        [
            jnp.zeros_like(lax.slice_in_dim(array, 0, 1, axis=dim_index)),
            lax.slice_in_dim(array, 0, length - 1, axis=dim_index),
        ],
        axis=dim_index,
    )
    return array - previous


def depth_forward(array, plane_high):
    following = jnp.concatenate([array[:, 1:], plane_high[:, None]], axis=1)
    return following - array


def depth_backward(array, plane_low):
    previous = jnp.concatenate([plane_low[:, None], array[:, :-1]], axis=1)
    return array - previous


def velocity_half(fields, buoyancy, sxz_low, syz_low, szz_high):
    vel_x, vel_y, vel_z, sig_xx, sig_yy, sig_zz, sig_xy, sig_xz, sig_yz = fields
    vel_x = vel_x + time_step * buoyancy * (
        forward_diff(sig_xx, 2) + backward_diff(sig_xy, 3) + depth_backward(sig_xz, sxz_low)
    )
    vel_y = vel_y + time_step * buoyancy * (
        backward_diff(sig_xy, 2) + forward_diff(sig_yy, 3) + depth_backward(sig_yz, syz_low)
    )
    vel_z = vel_z + time_step * buoyancy * (
        backward_diff(sig_xz, 2) + backward_diff(sig_yz, 3) + depth_forward(sig_zz, szz_high)
    )
    return (vel_x, vel_y, vel_z)


def stress_half(fields, lame_lambda, shear_mu, vz_low, vx_high, vy_high):
    vel_x, vel_y, vel_z, sig_xx, sig_yy, sig_zz, sig_xy, sig_xz, sig_yz = fields
    strain_x = backward_diff(vel_x, 2)
    strain_y = backward_diff(vel_y, 3)
    strain_z = depth_backward(vel_z, vz_low)
    spread = strain_x + strain_y + strain_z
    sig_xx = sig_xx + time_step * (lame_lambda * spread + 2.0 * shear_mu * strain_x)
    sig_yy = sig_yy + time_step * (lame_lambda * spread + 2.0 * shear_mu * strain_y)
    sig_zz = sig_zz + time_step * (lame_lambda * spread + 2.0 * shear_mu * strain_z)
    vx_up = depth_forward(vel_x, vx_high)
    vy_up = depth_forward(vel_y, vy_high)
    vz_along_x = forward_diff(vel_z, 2)
    vz_along_y = forward_diff(vel_z, 3)
    vx_along_y = forward_diff(vel_x, 3)
    vy_along_x = forward_diff(vel_y, 2)
    sig_xy = sig_xy + time_step * shear_mu * (vx_along_y + vy_along_x)
    sig_xz = sig_xz + time_step * shear_mu * (vx_up + vz_along_x)
    sig_yz = sig_yz + time_step * shear_mu * (vy_up + vz_along_y)
    rotation = vz_along_y - vy_up + (vx_up - vz_along_x) + (vy_along_x - vx_along_y)
    return ([vel_x, vel_y, vel_z, sig_xx, sig_yy, sig_zz, sig_xy, sig_xz, sig_yz], rotation)


def add_points(field_in, wave_index, depth_at, row_index, col_index, amounts, limit_at):
    inside = (depth_at >= 0) & (depth_at < limit_at)
    place_at = jnp.where(inside, depth_at, limit_at)
    return field_in.at[wave_index, place_at, row_index, col_index].add(amounts, mode="drop")


def advance(fields, material, receiver_add, source_add):
    stress_lows = shifted(jnp.stack([fields[7][:, -1], fields[8][:, -1]]), "gz", 1)
    sxz_low = stress_lows[0]
    syz_low = stress_lows[1]
    szz_high = shifted(fields[5][:, 0], "gz", -1)
    vel_x, vel_y, vel_z = velocity_half(fields, material[0], sxz_low, syz_low, szz_high)
    vel_z = receiver_add(vel_z)
    vz_low = shifted(vel_z[:, -1], "gz", 1)
    vel_highs = shifted(jnp.stack([vel_x[:, 0], vel_y[:, 0]]), "gz", -1)
    vx_high = vel_highs[0]
    vy_high = vel_highs[1]
    updated, rotation = stress_half(
        [vel_x, vel_y, vel_z] + list(fields[3:]), material[1], material[2], vz_low, vx_high, vy_high
    )
    for field_no in (3, 4, 5):
        updated[field_no] = source_add(updated[field_no])
    return (updated, rotation)


def on_device(
    wavefields,
    earth_model,
    source_depth,
    source_column,
    wavelet,
    receiver_depth,
    receiver_column,
    traces,
):
    fields_now = wavefields[0]
    slab_depth = fields_now.shape[2]
    width_y = fields_now.shape[4]
    steps_total = wavelet.shape[1]
    offset = lax.axis_index("gz") * slab_depth
    src_row = source_column[0] // width_y
    src_col = source_column[0] % width_y
    rec_row = receiver_column[0] // width_y
    rec_col = receiver_column[0] % width_y
    tallies = {
        "image_pp": jnp.zeros(fields_now.shape[2:], jnp.float32),
        "image_ps": jnp.zeros(fields_now.shape[2:], jnp.float32),
        "first_half": None,
    }

    def tally(pressure, rotation):
        tallies["image_pp"] = tallies["image_pp"] + pressure[0] * pressure[1]
        tallies["image_ps"] = tallies["image_ps"] + pressure[0] * rotation[1]

    def injectors(step_index, limit_at):

        def receiver_add(vel_z):
            return add_points(
                vel_z,
                1,
                receiver_depth[0] - offset,
                rec_row,
                rec_col,
                time_step * traces[0, step_index],
                limit_at,
            )

        def source_add(normal):
            return add_points(
                normal,
                0,
                source_depth[0] - offset,
                src_row,
                src_col,
                time_step * wavelet[0, step_index],
                limit_at,
            )

        return (receiver_add, source_add)

    fields = [fields_now[:, field_no] for field_no in range(9)]
    for step_index in range(steps_total):
        receiver_add, source_add = injectors(step_index, slab_depth)
        fields, rotation = advance(fields, earth_model, receiver_add, source_add)
        pressure = (fields[3] + fields[4] + fields[5]) / 3.0
        tally(pressure, rotation)
    summed_pp, summed_ps = lax.psum((tallies["image_pp"], tallies["image_ps"]), "shot")
    return jnp.stack([summed_pp, summed_ps]) / steps_total


def solution(mesh):
    placed = (
        P(("parts", "shot"), None, None, "gz", None, None),
        P("parts", "gz", None, None),
        P(("parts", "shot")),
        P(("parts", "shot")),
        P(("parts", "shot"), None),
        P(("parts", "shot"), None),
        P(("parts", "shot"), None),
        P(("parts", "shot"), None, None),
    )
    return jax.shard_map(
        on_device,
        mesh=mesh,
        in_specs=placed,
        out_specs=P("parts", "gz", None, None),
        check_vma=False,
    )
```

profile of v0, /device:TPU:0, one launch (start us, length us, event | category | flops | bytes accessed | tf_op | source)
XLA Modules:
  0.0 302.1 jit_solution(4630040369548691662)
XLA Ops:
  8.1 5.0 %collective-permute-start = (f32[2,2,32,128]{3,2,1,0:T(8,128)S(1)}, f32[2,2,32,128]{3,2,1,0:T(8,128)S(1)}, u32[]{:S(2)}, u32[]{:S(2)}) collective-permute-start(f32[2,2,32,128]{3,2,1,0:T(8,128)S(1)} %pad_maximum_fusion.2), channel_id=1, source_target_pairs={{0,4},{4,8},{8,12},{1,5},{5,9},{9,13},{2,6},{6,10},{10,14},{3,7},{... | collective-permute-start | bytes 196616 | tf_op jit(solution)/shard_map/ppermute | solution.py:12
  24.2 5.3 %scatter_fusion = f32[2,4,32,128]{3,2,1,0:T(8,128)S(1)} fusion(f32[2,4,32,128]{3,2,1,0:T(8,128)S(1)} %copy.13, s32[64]{0:T(128)S(1)} %fusion.121, f32[64]{0:T(128)S(1)} %get-tuple-element.516), kind=kCustom, calls=%fused_computation | custom fusion | flops 64 | bytes 1792 | tf_op jit(solution)/shard_map/scatter-add | solution.py:88
  29.8 5.2 %collective-permute-start.2 = (f32[2,32,128]{2,1,0:T(8,128)S(1)}, f32[2,32,128]{2,1,0:T(8,128)S(1)}, u32[]{:S(2)}, u32[]{:S(2)}) collective-permute-start(f32[2,32,128]{2,1,0:T(8,128)S(1)} %slice_bitcast_fusion.84), channel_id=1, source_target_pairs={{0,4},{4,8},{8,12},{1,5},{5,9},{9,13},{2,6},{6,10},{10,14},{3,7},{... | collective-permute-start | bytes 98312 | tf_op jit(solution)/shard_map/ppermute | solution.py:12
  35.1 1.5 collective-permute-done.2
  38.4 4.2 %collective-permute-start.4 = (f32[2,2,32,128]{3,2,1,0:T(8,128)S(1)}, f32[2,2,32,128]{3,2,1,0:T(8,128)S(1)}, u32[]{:S(2)}, u32[]{:S(2)}) collective-permute-start(f32[2,2,32,128]{3,2,1,0:T(8,128)S(1)} %pad_maximum_fusion.4), channel_id=1, source_target_pairs={{0,4},{4,8},{8,12},{1,5},{5,9},{9,13},{2,6},{6,10},{10,14},{3,7},{... | collective-permute-start | bytes 196616 | tf_op jit(solution)/shard_map/ppermute | solution.py:12
  53.6 2.9 collective-permute-done.5
  56.6 5.3 %scatter_fusion.1 = f32[2,4,32,128]{3,2,1,0:T(8,128)S(1)} fusion(f32[2,4,32,128]{3,2,1,0:T(8,128)S(1)} %fusion.17, s32[64]{0:T(128)S(1)} %fusion.121, f32[64]{0:T(128)S(1)} %get-tuple-element.515), kind=kCustom, calls=%fused_computation.1 | custom fusion | flops 64 | bytes 1792 | tf_op jit(solution)/shard_map/scatter-add | solution.py:88
  62.2 3.9 %collective-permute-start.6 = (f32[2,32,128]{2,1,0:T(8,128)S(1)}, f32[2,32,128]{2,1,0:T(8,128)S(1)}, u32[]{:S(2)}, u32[]{:S(2)}) collective-permute-start(f32[2,32,128]{2,1,0:T(8,128)S(1)} %slice_bitcast_fusion.74), channel_id=1, source_target_pairs={{0,4},{4,8},{8,12},{1,5},{5,9},{9,13},{2,6},{6,10},{10,14},{3,7},{... | collective-permute-start | bytes 98312 | tf_op jit(solution)/shard_map/ppermute | solution.py:12
  79.2 4.9 %collective-permute-start.8 = (f32[2,2,32,128]{3,2,1,0:T(8,128)S(1)}, f32[2,2,32,128]{3,2,1,0:T(8,128)S(1)}, u32[]{:S(2)}, u32[]{:S(2)}) collective-permute-start(f32[2,2,32,128]{3,2,1,0:T(8,128)S(1)} %pad_maximum_fusion.6), channel_id=1, source_target_pairs={{0,4},{4,8},{8,12},{1,5},{5,9},{9,13},{2,6},{6,10},{10,14},{3,7},{... | collective-permute-start | bytes 196616 | tf_op jit(solution)/shard_map/ppermute | solution.py:12
  84.2 5.3 %scatter_fusion.2 = f32[2,4,32,128]{3,2,1,0:T(8,128)S(1)} fusion(f32[2,4,32,128]{3,2,1,0:T(8,128)S(1)} %copy.52, s32[64]{0:T(128)S(1)} %fusion.121, f32[64]{0:T(128)S(1)} %get-tuple-element.514), kind=kCustom, calls=%fused_computation.2 | custom fusion | flops 64 | bytes 1792 | tf_op jit(solution)/shard_map/scatter-add | solution.py:88
  91.3 4.6 %collective-permute-start.10 = (f32[2,32,128]{2,1,0:T(8,128)S(1)}, f32[2,32,128]{2,1,0:T(8,128)S(1)}, u32[]{:S(2)}, u32[]{:S(2)}) collective-permute-start(f32[2,32,128]{2,1,0:T(8,128)S(1)} %slice_bitcast_fusion.64), channel_id=1, source_target_pairs={{0,4},{4,8},{8,12},{1,5},{5,9},{9,13},{2,6},{6,10},{10,14},{3,7},{... | collective-permute-start | bytes 98312 | tf_op jit(solution)/shard_map/ppermute | solution.py:12
  109.0 5.0 %collective-permute-start.12 = (f32[2,2,32,128]{3,2,1,0:T(8,128)S(1)}, f32[2,2,32,128]{3,2,1,0:T(8,128)S(1)}, u32[]{:S(2)}, u32[]{:S(2)}) collective-permute-start(f32[2,2,32,128]{3,2,1,0:T(8,128)S(1)} %pad_maximum_fusion.8), channel_id=1, source_target_pairs={{0,4},{4,8},{8,12},{1,5},{5,9},{9,13},{2,6},{6,10},{10,14},{3,7},{... | collective-permute-start | bytes 196616 | tf_op jit(solution)/shard_map/ppermute | solution.py:12
  114.3 5.3 %scatter_fusion.3 = f32[2,4,32,128]{3,2,1,0:T(8,128)S(1)} fusion(f32[2,4,32,128]{3,2,1,0:T(8,128)S(1)} %copy.74, s32[64]{0:T(128)S(1)} %fusion.121, f32[64]{0:T(128)S(1)} %get-tuple-element.513), kind=kCustom, calls=%fused_computation.3 | custom fusion | flops 64 | bytes 1792 | tf_op jit(solution)/shard_map/scatter-add | solution.py:88
  121.3 4.6 %collective-permute-start.14 = (f32[2,32,128]{2,1,0:T(8,128)S(1)}, f32[2,32,128]{2,1,0:T(8,128)S(1)}, u32[]{:S(2)}, u32[]{:S(2)}) collective-permute-start(f32[2,32,128]{2,1,0:T(8,128)S(1)} %slice_bitcast_fusion.54), channel_id=1, source_target_pairs={{0,4},{4,8},{8,12},{1,5},{5,9},{9,13},{2,6},{6,10},{10,14},{3,7},{... | collective-permute-start | bytes 98312 | tf_op jit(solution)/shard_map/ppermute | solution.py:12
  132.1 4.2 %collective-permute-start.16 = (f32[2,2,32,128]{3,2,1,0:T(8,128)S(1)}, f32[2,2,32,128]{3,2,1,0:T(8,128)S(1)}, u32[]{:S(2)}, u32[]{:S(2)}) collective-permute-start(f32[2,2,32,128]{3,2,1,0:T(8,128)S(1)} %pad_maximum_fusion.10), channel_id=1, source_target_pairs={{0,4},{4,8},{8,12},{1,5},{5,9},{9,13},{2,6},{6,10},{10,14},{3,7},{... | collective-permute-start | bytes 196616 | tf_op jit(solution)/shard_map/ppermute | solution.py:12
  143.3 1.7 collective-permute-done.17
  145.2 5.3 %scatter_fusion.4 = f32[2,4,32,128]{3,2,1,0:T(8,128)S(1)} fusion(f32[2,4,32,128]{3,2,1,0:T(8,128)S(1)} %copy.100, s32[64]{0:T(128)S(1)} %fusion.121, f32[64]{0:T(128)S(1)} %get-tuple-element.512), kind=kCustom, calls=%fused_computation.4 | custom fusion | flops 64 | bytes 1792 | tf_op jit(solution)/shard_map/scatter-add | solution.py:88
  150.5 3.9 %collective-permute-start.18 = (f32[2,32,128]{2,1,0:T(8,128)S(1)}, f32[2,32,128]{2,1,0:T(8,128)S(1)}, u32[]{:S(2)}, u32[]{:S(2)}) collective-permute-start(f32[2,32,128]{2,1,0:T(8,128)S(1)} %slice_bitcast_fusion.44), channel_id=1, source_target_pairs={{0,4},{4,8},{8,12},{1,5},{5,9},{9,13},{2,6},{6,10},{10,14},{3,7},{... | collective-permute-start | bytes 98312 | tf_op jit(solution)/shard_map/ppermute | solution.py:12
  161.9 5.2 %collective-permute-start.20 = (f32[2,2,32,128]{3,2,1,0:T(8,128)S(1)}, f32[2,2,32,128]{3,2,1,0:T(8,128)S(1)}, u32[]{:S(2)}, u32[]{:S(2)}) collective-permute-start(f32[2,2,32,128]{3,2,1,0:T(8,128)S(1)} %pad_maximum_fusion.12), channel_id=1, source_target_pairs={{0,4},{4,8},{8,12},{1,5},{5,9},{9,13},{2,6},{6,10},{10,14},{3,7},{... | collective-permute-start | bytes 196616 | tf_op jit(solution)/shard_map/ppermute | solution.py:12
  174.6 5.3 %scatter_fusion.5 = f32[2,4,32,128]{3,2,1,0:T(8,128)S(1)} fusion(f32[2,4,32,128]{3,2,1,0:T(8,128)S(1)} %get-tuple-element.429, s32[64]{0:T(128)S(1)} %fusion.121, f32[64]{0:T(128)S(1)} %get-tuple-element.511), kind=kCustom, calls=%fused_computation.5 | custom fusion | flops 64 | bytes 1792 | tf_op jit(solution)/shard_map/scatter-add | solution.py:88
  180.2 4.6 %collective-permute-start.22 = (f32[2,32,128]{2,1,0:T(8,128)S(1)}, f32[2,32,128]{2,1,0:T(8,128)S(1)}, u32[]{:S(2)}, u32[]{:S(2)}) collective-permute-start(f32[2,32,128]{2,1,0:T(8,128)S(1)} %slice_bitcast_fusion.34), channel_id=1, source_target_pairs={{0,4},{4,8},{8,12},{1,5},{5,9},{9,13},{2,6},{6,10},{10,14},{3,7},{... | collective-permute-start | bytes 98312 | tf_op jit(solution)/shard_map/ppermute | solution.py:12
  188.3 4.2 %collective-permute-start.24 = (f32[2,2,32,128]{3,2,1,0:T(8,128)S(1)}, f32[2,2,32,128]{3,2,1,0:T(8,128)S(1)}, u32[]{:S(2)}, u32[]{:S(2)}) collective-permute-start(f32[2,2,32,128]{3,2,1,0:T(8,128)S(1)} %pad_maximum_fusion.14), channel_id=1, source_target_pairs={{0,4},{4,8},{8,12},{1,5},{5,9},{9,13},{2,6},{6,10},{10,14},{3,7},{... | collective-permute-start | bytes 196616 | tf_op jit(solution)/shard_map/ppermute | solution.py:12
  203.6 3.0 %collective-permute-done.25 = f32[2,32,128]{2,1,0:T(8,128)S(1)} collective-permute-done((f32[2,32,128]{2,1,0:T(8,128)S(1)}, f32[2,32,128]{2,1,0:T(8,128)S(1)}, u32[]{:S(2)}, u32[]{:S(2)}) %collective-permute-start.25) | collective-permute-done | bytes 32800 | tf_op jit(solution)/shard_map/ppermute | solution.py:12
  206.7 5.3 %scatter_fusion.6 = f32[2,4,32,128]{3,2,1,0:T(8,128)S(1)} fusion(f32[2,4,32,128]{3,2,1,0:T(8,128)S(1)} %copy.156, s32[64]{0:T(128)S(1)} %fusion.121, f32[64]{0:T(128)S(1)} %get-tuple-element.517), kind=kCustom, calls=%fused_computation.6 | custom fusion | flops 64 | bytes 1792 | tf_op jit(solution)/shard_map/scatter-add | solution.py:88
  212.2 3.9 %collective-permute-start.26 = (f32[2,32,128]{2,1,0:T(8,128)S(1)}, f32[2,32,128]{2,1,0:T(8,128)S(1)}, u32[]{:S(2)}, u32[]{:S(2)}) collective-permute-start(f32[2,32,128]{2,1,0:T(8,128)S(1)} %slice_bitcast_fusion.24), channel_id=1, source_target_pairs={{0,4},{4,8},{8,12},{1,5},{5,9},{9,13},{2,6},{6,10},{10,14},{3,7},{... | collective-permute-start | bytes 98312 | tf_op jit(solution)/shard_map/ppermute | solution.py:12
  219.6 4.4 %collective-permute-start.28 = (f32[2,2,32,128]{3,2,1,0:T(8,128)S(1)}, f32[2,2,32,128]{3,2,1,0:T(8,128)S(1)}, u32[]{:S(2)}, u32[]{:S(2)}) collective-permute-start(f32[2,2,32,128]{3,2,1,0:T(8,128)S(1)} %pad_maximum_fusion.16), channel_id=1, source_target_pairs={{0,4},{4,8},{8,12},{1,5},{5,9},{9,13},{2,6},{6,10},{10,14},{3,7},{... | collective-permute-start | bytes 196616 | tf_op jit(solution)/shard_map/ppermute | solution.py:12
  233.7 4.3 %collective-permute-done.29 = f32[2,32,128]{2,1,0:T(8,128)S(1)} collective-permute-done((f32[2,32,128]{2,1,0:T(8,128)S(1)}, f32[2,32,128]{2,1,0:T(8,128)S(1)}, u32[]{:S(2)}, u32[]{:S(2)}) %collective-permute-start.29) | collective-permute-done | bytes 32800 | tf_op jit(solution)/shard_map/ppermute | solution.py:12
  238.4 5.3 %scatter_fusion.7 = f32[2,4,32,128]{3,2,1,0:T(8,128)S(1)} fusion(f32[2,4,32,128]{3,2,1,0:T(8,128)S(1)} %get-tuple-element.417, s32[64]{0:T(128)S(1)} %fusion.121, f32[64]{0:T(128)S(1)} %get-tuple-element.510), kind=kCustom, calls=%fused_computation.7 | custom fusion | flops 64 | bytes 1792 | tf_op jit(solution)/shard_map/scatter-add | solution.py:88
  243.7 3.9 %collective-permute-start.30 = (f32[2,32,128]{2,1,0:T(8,128)S(1)}, f32[2,32,128]{2,1,0:T(8,128)S(1)}, u32[]{:S(2)}, u32[]{:S(2)}) collective-permute-start(f32[2,32,128]{2,1,0:T(8,128)S(1)} %slice_bitcast_fusion.14), channel_id=1, source_target_pairs={{0,4},{4,8},{8,12},{1,5},{5,9},{9,13},{2,6},{6,10},{10,14},{3,7},{... | collective-permute-start | bytes 98312 | tf_op jit(solution)/shard_map/ppermute | solution.py:12
  259.5 2.8 fusion.80
  262.4 31.4 %all-reduce.99.cloned.1.call-done = (f32[1,4,32,128]{3,2,1,0:T(8,128)}, f32[1,4,32,128]{3,2,1,0:T(8,128)}) async-done(((f32[1,4,32,128]{3,2,1,0:T(8,128)}, f32[1,4,32,128]{3,2,1,0:T(8,128)}), (f32[1,4,32,128]{3,2,1,0:T(8,128)}, f32[1,4,32,128]{3,2,1,0:T(8,128)})) %all-reduce.99.cloned.1.call-update) | async-done | bytes 131088 | tf_op jit(solution)/shard_map/psum | solution.py:171
  293.8 1.5 maximum_multiply_fusion
  (381 shorter events, 71.7 us)
Async XLA Ops:
  6.5 287.2 %all-reduce.99.cloned.1.call-start = ((), (), s32[]{:S(2)}) async-start(), calls=%async_computation | async-start | bytes 262144 | tf_op jit(solution)/shard_map/psum | solution.py:171
  8.1 14.4 %collective-permute-start = (f32[2,2,32,128]{3,2,1,0:T(8,128)S(1)}, f32[2,2,32,128]{3,2,1,0:T(8,128)S(1)}, u32[]{:S(2)}, u32[]{:S(2)}) collective-permute-start(f32[2,2,32,128]{3,2,1,0:T(8,128)S(1)} %pad_maximum_fusion.2), channel_id=1, source_target_pairs={{0,4},{4,8},{8,12},{1,5},{5,9},{9,13},{2,6},{6,10},{10,14},{3,7},{... | collective-permute-start | bytes 196616 | tf_op jit(solution)/shard_map/ppermute | solution.py:12
  13.1 9.4 %collective-permute-start.1 = (f32[2,32,128]{2,1,0:T(8,128)S(1)}, f32[2,32,128]{2,1,0:T(8,128)S(1)}, u32[]{:S(2)}, u32[]{:S(2)}) collective-permute-start(f32[2,32,128]{2,1,0:T(8,128)S(1)} %slice_bitcast_fusion.85), channel_id=1, source_target_pairs={{4,0},{8,4},{12,8},{5,1},{9,5},{13,9},{6,2},{10,6},{14,10},{7,3},{... | collective-permute-start | bytes 98312 | tf_op jit(solution)/shard_map/ppermute | solution.py:12
  22.9 12.2 %collective-permute-start.3 = (f32[2,2,32,128]{3,2,1,0:T(8,128)S(1)}, f32[2,2,32,128]{3,2,1,0:T(8,128)S(1)}, u32[]{:S(2)}, u32[]{:S(2)}) collective-permute-start(f32[2,2,32,128]{3,2,1,0:T(8,128)S(1)} %pad_maximum_fusion.3), channel_id=1, source_target_pairs={{4,0},{8,4},{12,8},{5,1},{9,5},{13,9},{6,2},{10,6},{14,10},{7,3},{... | collective-permute-start | bytes 196616 | tf_op jit(solution)/shard_map/ppermute | solution.py:12
  29.8 6.8 %collective-permute-start.2 = (f32[2,32,128]{2,1,0:T(8,128)S(1)}, f32[2,32,128]{2,1,0:T(8,128)S(1)}, u32[]{:S(2)}, u32[]{:S(2)}) collective-permute-start(f32[2,32,128]{2,1,0:T(8,128)S(1)} %slice_bitcast_fusion.84), channel_id=1, source_target_pairs={{0,4},{4,8},{8,12},{1,5},{5,9},{9,13},{2,6},{6,10},{10,14},{3,7},{... | collective-permute-start | bytes 98312 | tf_op jit(solution)/shard_map/ppermute | solution.py:12
  38.4 13.6 %collective-permute-start.4 = (f32[2,2,32,128]{3,2,1,0:T(8,128)S(1)}, f32[2,2,32,128]{3,2,1,0:T(8,128)S(1)}, u32[]{:S(2)}, u32[]{:S(2)}) collective-permute-start(f32[2,2,32,128]{3,2,1,0:T(8,128)S(1)} %pad_maximum_fusion.4), channel_id=1, source_target_pairs={{0,4},{4,8},{8,12},{1,5},{5,9},{9,13},{2,6},{6,10},{10,14},{3,7},{... | collective-permute-start | bytes 196616 | tf_op jit(solution)/shard_map/ppermute | solution.py:12
  50.7 5.8 %collective-permute-start.5 = (f32[2,32,128]{2,1,0:T(8,128)S(1)}, f32[2,32,128]{2,1,0:T(8,128)S(1)}, u32[]{:S(2)}, u32[]{:S(2)}) collective-permute-start(f32[2,32,128]{2,1,0:T(8,128)S(1)} %slice_bitcast_fusion.75), channel_id=1, source_target_pairs={{4,0},{8,4},{12,8},{5,1},{9,5},{13,9},{6,2},{10,6},{14,10},{7,3},{... | collective-permute-start | bytes 98312 | tf_op jit(solution)/shard_map/ppermute | solution.py:12
  52.3 13.8 %collective-permute-start.7 = (f32[2,2,32,128]{3,2,1,0:T(8,128)S(1)}, f32[2,2,32,128]{3,2,1,0:T(8,128)S(1)}, u32[]{:S(2)}, u32[]{:S(2)}) collective-permute-start(f32[2,2,32,128]{3,2,1,0:T(8,128)S(1)} %pad_maximum_fusion.5), channel_id=1, source_target_pairs={{4,0},{8,4},{12,8},{5,1},{9,5},{13,9},{6,2},{10,6},{14,10},{7,3},{... | collective-permute-start | bytes 196616 | tf_op jit(solution)/shard_map/ppermute | solution.py:12
  62.2 5.5 %collective-permute-start.6 = (f32[2,32,128]{2,1,0:T(8,128)S(1)}, f32[2,32,128]{2,1,0:T(8,128)S(1)}, u32[]{:S(2)}, u32[]{:S(2)}) collective-permute-start(f32[2,32,128]{2,1,0:T(8,128)S(1)} %slice_bitcast_fusion.74), channel_id=1, source_target_pairs={{0,4},{4,8},{8,12},{1,5},{5,9},{9,13},{2,6},{6,10},{10,14},{3,7},{... | collective-permute-start | bytes 98312 | tf_op jit(solution)/shard_map/ppermute | solution.py:12
  72.3 11.8 %collective-permute-start.9 = (f32[2,32,128]{2,1,0:T(8,128)S(1)}, f32[2,32,128]{2,1,0:T(8,128)S(1)}, u32[]{:S(2)}, u32[]{:S(2)}) collective-permute-start(f32[2,32,128]{2,1,0:T(8,128)S(1)} %slice_bitcast_fusion.65), channel_id=1, source_target_pairs={{4,0},{8,4},{12,8},{5,1},{9,5},{13,9},{6,2},{10,6},{14,10},{7,3},{... | collective-permute-start | bytes 98312 | tf_op jit(solution)/shard_map/ppermute | solution.py:12
  79.2 10.3 %collective-permute-start.8 = (f32[2,2,32,128]{3,2,1,0:T(8,128)S(1)}, f32[2,2,32,128]{3,2,1,0:T(8,128)S(1)}, u32[]{:S(2)}, u32[]{:S(2)}) collective-permute-start(f32[2,2,32,128]{3,2,1,0:T(8,128)S(1)} %pad_maximum_fusion.6), channel_id=1, source_target_pairs={{0,4},{4,8},{8,12},{1,5},{5,9},{9,13},{2,6},{6,10},{10,14},{3,7},{... | collective-permute-start | bytes 196616 | tf_op jit(solution)/shard_map/ppermute | solution.py:12
  89.8 6.2 %collective-permute-start.11 = (f32[2,2,32,128]{3,2,1,0:T(8,128)S(1)}, f32[2,2,32,128]{3,2,1,0:T(8,128)S(1)}, u32[]{:S(2)}, u32[]{:S(2)}) collective-permute-start(f32[2,2,32,128]{3,2,1,0:T(8,128)S(1)} %pad_maximum_fusion.7), channel_id=1, source_target_pairs={{4,0},{8,4},{12,8},{5,1},{9,5},{13,9},{6,2},{10,6},{14,10},{7,3},{... | collective-permute-start | bytes 196616 | tf_op jit(solution)/shard_map/ppermute | solution.py:12
  91.3 6.2 %collective-permute-start.10 = (f32[2,32,128]{2,1,0:T(8,128)S(1)}, f32[2,32,128]{2,1,0:T(8,128)S(1)}, u32[]{:S(2)}, u32[]{:S(2)}) collective-permute-start(f32[2,32,128]{2,1,0:T(8,128)S(1)} %slice_bitcast_fusion.64), channel_id=1, source_target_pairs={{0,4},{4,8},{8,12},{1,5},{5,9},{9,13},{2,6},{6,10},{10,14},{3,7},{... | collective-permute-start | bytes 98312 | tf_op jit(solution)/shard_map/ppermute | solution.py:12
  102.1 12.0 %collective-permute-start.13 = (f32[2,32,128]{2,1,0:T(8,128)S(1)}, f32[2,32,128]{2,1,0:T(8,128)S(1)}, u32[]{:S(2)}, u32[]{:S(2)}) collective-permute-start(f32[2,32,128]{2,1,0:T(8,128)S(1)} %slice_bitcast_fusion.55), channel_id=1, source_target_pairs={{4,0},{8,4},{12,8},{5,1},{9,5},{13,9},{6,2},{10,6},{14,10},{7,3},{... | collective-permute-start | bytes 98312 | tf_op jit(solution)/shard_map/ppermute | solution.py:12
  109.0 10.5 %collective-permute-start.12 = (f32[2,2,32,128]{3,2,1,0:T(8,128)S(1)}, f32[2,2,32,128]{3,2,1,0:T(8,128)S(1)}, u32[]{:S(2)}, u32[]{:S(2)}) collective-permute-start(f32[2,2,32,128]{3,2,1,0:T(8,128)S(1)} %pad_maximum_fusion.8), channel_id=1, source_target_pairs={{0,4},{4,8},{8,12},{1,5},{5,9},{9,13},{2,6},{6,10},{10,14},{3,7},{... | collective-permute-start | bytes 196616 | tf_op jit(solution)/shard_map/ppermute | solution.py:12
  119.8 6.2 %collective-permute-start.15 = (f32[2,2,32,128]{3,2,1,0:T(8,128)S(1)}, f32[2,2,32,128]{3,2,1,0:T(8,128)S(1)}, u32[]{:S(2)}, u32[]{:S(2)}) collective-permute-start(f32[2,2,32,128]{3,2,1,0:T(8,128)S(1)} %pad_maximum_fusion.9), channel_id=1, source_target_pairs={{4,0},{8,4},{12,8},{5,1},{9,5},{13,9},{6,2},{10,6},{14,10},{7,3},{... | collective-permute-start | bytes 196616 | tf_op jit(solution)/shard_map/ppermute | solution.py:12
  121.3 6.2 %collective-permute-start.14 = (f32[2,32,128]{2,1,0:T(8,128)S(1)}, f32[2,32,128]{2,1,0:T(8,128)S(1)}, u32[]{:S(2)}, u32[]{:S(2)}) collective-permute-start(f32[2,32,128]{2,1,0:T(8,128)S(1)} %slice_bitcast_fusion.54), channel_id=1, source_target_pairs={{0,4},{4,8},{8,12},{1,5},{5,9},{9,13},{2,6},{6,10},{10,14},{3,7},{... | collective-permute-start | bytes 98312 | tf_op jit(solution)/shard_map/ppermute | solution.py:12
  132.1 11.2 %collective-permute-start.16 = (f32[2,2,32,128]{3,2,1,0:T(8,128)S(1)}, f32[2,2,32,128]{3,2,1,0:T(8,128)S(1)}, u32[]{:S(2)}, u32[]{:S(2)}) collective-permute-start(f32[2,2,32,128]{3,2,1,0:T(8,128)S(1)} %pad_maximum_fusion.10), channel_id=1, source_target_pairs={{0,4},{4,8},{8,12},{1,5},{5,9},{9,13},{2,6},{6,10},{10,14},{3,7},{... | collective-permute-start | bytes 196616 | tf_op jit(solution)/shard_map/ppermute | solution.py:12
  139.1 5.8 %collective-permute-start.17 = (f32[2,32,128]{2,1,0:T(8,128)S(1)}, f32[2,32,128]{2,1,0:T(8,128)S(1)}, u32[]{:S(2)}, u32[]{:S(2)}) collective-permute-start(f32[2,32,128]{2,1,0:T(8,128)S(1)} %slice_bitcast_fusion.45), channel_id=1, source_target_pairs={{4,0},{8,4},{12,8},{5,1},{9,5},{13,9},{6,2},{10,6},{14,10},{7,3},{... | collective-permute-start | bytes 98312 | tf_op jit(solution)/shard_map/ppermute | solution.py:12
  150.5 5.6 %collective-permute-start.18 = (f32[2,32,128]{2,1,0:T(8,128)S(1)}, f32[2,32,128]{2,1,0:T(8,128)S(1)}, u32[]{:S(2)}, u32[]{:S(2)}) collective-permute-start(f32[2,32,128]{2,1,0:T(8,128)S(1)} %slice_bitcast_fusion.44), channel_id=1, source_target_pairs={{0,4},{4,8},{8,12},{1,5},{5,9},{9,13},{2,6},{6,10},{10,14},{3,7},{... | collective-permute-start | bytes 98312 | tf_op jit(solution)/shard_map/ppermute | solution.py:12
  154.8 6.2 %collective-permute-start.19 = (f32[2,2,32,128]{3,2,1,0:T(8,128)S(1)}, f32[2,2,32,128]{3,2,1,0:T(8,128)S(1)}, u32[]{:S(2)}, u32[]{:S(2)}) collective-permute-start(f32[2,2,32,128]{3,2,1,0:T(8,128)S(1)} %pad_maximum_fusion.11), channel_id=1, source_target_pairs={{4,0},{8,4},{12,8},{5,1},{9,5},{13,9},{6,2},{10,6},{14,10},{7,3},{... | collective-permute-start | bytes 196616 | tf_op jit(solution)/shard_map/ppermute | solution.py:12
  159.7 13.2 %collective-permute-start.21 = (f32[2,32,128]{2,1,0:T(8,128)S(1)}, f32[2,32,128]{2,1,0:T(8,128)S(1)}, u32[]{:S(2)}, u32[]{:S(2)}) collective-permute-start(f32[2,32,128]{2,1,0:T(8,128)S(1)} %slice_bitcast_fusion.35), channel_id=1, source_target_pairs={{4,0},{8,4},{12,8},{5,1},{9,5},{13,9},{6,2},{10,6},{14,10},{7,3},{... | collective-permute-start | bytes 98312 | tf_op jit(solution)/shard_map/ppermute | solution.py:12
  161.9 10.9 %collective-permute-start.20 = (f32[2,2,32,128]{3,2,1,0:T(8,128)S(1)}, f32[2,2,32,128]{3,2,1,0:T(8,128)S(1)}, u32[]{:S(2)}, u32[]{:S(2)}) collective-permute-start(f32[2,2,32,128]{3,2,1,0:T(8,128)S(1)} %pad_maximum_fusion.12), channel_id=1, source_target_pairs={{0,4},{4,8},{8,12},{1,5},{5,9},{9,13},{2,6},{6,10},{10,14},{3,7},{... | collective-permute-start | bytes 196616 | tf_op jit(solution)/shard_map/ppermute | solution.py:12
  173.3 11.5 %collective-permute-start.23 = (f32[2,2,32,128]{3,2,1,0:T(8,128)S(1)}, f32[2,2,32,128]{3,2,1,0:T(8,128)S(1)}, u32[]{:S(2)}, u32[]{:S(2)}) collective-permute-start(f32[2,2,32,128]{3,2,1,0:T(8,128)S(1)} %pad_maximum_fusion.13), channel_id=1, source_target_pairs={{4,0},{8,4},{12,8},{5,1},{9,5},{13,9},{6,2},{10,6},{14,10},{7,3},{... | collective-permute-start | bytes 196616 | tf_op jit(solution)/shard_map/ppermute | solution.py:12
  180.2 6.2 %collective-permute-start.22 = (f32[2,32,128]{2,1,0:T(8,128)S(1)}, f32[2,32,128]{2,1,0:T(8,128)S(1)}, u32[]{:S(2)}, u32[]{:S(2)}) collective-permute-start(f32[2,32,128]{2,1,0:T(8,128)S(1)} %slice_bitcast_fusion.34), channel_id=1, source_target_pairs={{0,4},{4,8},{8,12},{1,5},{5,9},{9,13},{2,6},{6,10},{10,14},{3,7},{... | collective-permute-start | bytes 98312 | tf_op jit(solution)/shard_map/ppermute | solution.py:12
  188.3 12.2 %collective-permute-start.24 = (f32[2,2,32,128]{3,2,1,0:T(8,128)S(1)}, f32[2,2,32,128]{3,2,1,0:T(8,128)S(1)}, u32[]{:S(2)}, u32[]{:S(2)}) collective-permute-start(f32[2,2,32,128]{3,2,1,0:T(8,128)S(1)} %pad_maximum_fusion.14), channel_id=1, source_target_pairs={{0,4},{4,8},{8,12},{1,5},{5,9},{9,13},{2,6},{6,10},{10,14},{3,7},{... | collective-permute-start | bytes 196616 | tf_op jit(solution)/shard_map/ppermute | solution.py:12
  200.8 5.8 %collective-permute-start.25 = (f32[2,32,128]{2,1,0:T(8,128)S(1)}, f32[2,32,128]{2,1,0:T(8,128)S(1)}, u32[]{:S(2)}, u32[]{:S(2)}) collective-permute-start(f32[2,32,128]{2,1,0:T(8,128)S(1)} %slice_bitcast_fusion.25), channel_id=1, source_target_pairs={{4,0},{8,4},{12,8},{5,1},{9,5},{13,9},{6,2},{10,6},{14,10},{7,3},{... | collective-permute-start | bytes 98312 | tf_op jit(solution)/shard_map/ppermute | solution.py:12
  202.3 13.9 %collective-permute-start.27 = (f32[2,2,32,128]{3,2,1,0:T(8,128)S(1)}, f32[2,2,32,128]{3,2,1,0:T(8,128)S(1)}, u32[]{:S(2)}, u32[]{:S(2)}) collective-permute-start(f32[2,2,32,128]{3,2,1,0:T(8,128)S(1)} %pad_maximum_fusion.15), channel_id=1, source_target_pairs={{4,0},{8,4},{12,8},{5,1},{9,5},{13,9},{6,2},{10,6},{14,10},{7,3},{... | collective-permute-start | bytes 196616 | tf_op jit(solution)/shard_map/ppermute | solution.py:12
  219.6 12.4 %collective-permute-start.28 = (f32[2,2,32,128]{3,2,1,0:T(8,128)S(1)}, f32[2,2,32,128]{3,2,1,0:T(8,128)S(1)}, u32[]{:S(2)}, u32[]{:S(2)}) collective-permute-start(f32[2,2,32,128]{3,2,1,0:T(8,128)S(1)} %pad_maximum_fusion.16), channel_id=1, source_target_pairs={{0,4},{4,8},{8,12},{1,5},{5,9},{9,13},{2,6},{6,10},{10,14},{3,7},{... | collective-permute-start | bytes 196616 | tf_op jit(solution)/shard_map/ppermute | solution.py:12
  232.3 5.8 %collective-permute-start.29 = (f32[2,32,128]{2,1,0:T(8,128)S(1)}, f32[2,32,128]{2,1,0:T(8,128)S(1)}, u32[]{:S(2)}, u32[]{:S(2)}) collective-permute-start(f32[2,32,128]{2,1,0:T(8,128)S(1)} %slice_bitcast_fusion.15), channel_id=1, source_target_pairs={{4,0},{8,4},{12,8},{5,1},{9,5},{13,9},{6,2},{10,6},{14,10},{7,3},{... | collective-permute-start | bytes 98312 | tf_op jit(solution)/shard_map/ppermute | solution.py:12
  243.7 6.0 %collective-permute-start.30 = (f32[2,32,128]{2,1,0:T(8,128)S(1)}, f32[2,32,128]{2,1,0:T(8,128)S(1)}, u32[]{:S(2)}, u32[]{:S(2)}) collective-permute-start(f32[2,32,128]{2,1,0:T(8,128)S(1)} %slice_bitcast_fusion.14), channel_id=1, source_target_pairs={{0,4},{4,8},{8,12},{1,5},{5,9},{9,13},{2,6},{6,10},{10,14},{3,7},{... | collective-permute-start | bytes 98312 | tf_op jit(solution)/shard_map/ppermute | solution.py:12
  248.4 10.3 %collective-permute-start.31 = (f32[2,2,32,128]{3,2,1,0:T(8,128)}, f32[2,2,32,128]{3,2,1,0:T(8,128)}, u32[]{:S(2)}, u32[]{:S(2)}) collective-permute-start(f32[2,2,32,128]{3,2,1,0:T(8,128)} %pad_maximum_fusion.17), channel_id=1, source_target_pairs={{4,0},{8,4},{12,8},{5,1},{9,5},{13,9},{6,2},{10,6},{14,10},{7,3},{... | collective-permute-start | bytes 196616 | tf_op jit(solution)/shard_map/ppermute | solution.py:12
  (14 other events, 143.7 us)
Sparse Core Ops, SparseCore 0:
  262.5 31.1 all-reduce.98
where the time goes:
time: 304 us; the launch traced here: 302 us
  starting transfers between devices  92.4 us (30%)
  other arithmetic  77.9 us (26%)
  between operations  67.3 us (22%)
  waiting for transfers between devices  52.2 us (17%)
  local copies, waits for them, and re-layouts  12.3 us (4%)
    ppermute x32, starting transfers between devices, shifted(): lax.ppermute(value, axis, [(source, source + steps) for source in range(f...  92.4 us
    scatter-add x8, other arithmetic, add_points(): field_in.at[wave_index, place_at, row_index, col_index]  42.2 us
    psum x1, waiting for transfers between devices, on_device(): lax.psum((tallies['image_pp'], tallies['image_ps']), 'shot')  31.4 us
    ppermute x32, waiting for transfers between devices, shifted(): lax.ppermute(value, axis, [(source, source + steps) for source in range(f...  20.9 us
    add x20, other arithmetic, add_points(): field_in.at[wave_index, place_at, row_index, col_index]  13 us
  transfers between devices with their start and end apart: 33, of which 11 were waited for; matrix products, arithmetic and copies ran while one was open for 19% of the time, Pallas kernels for 0%

commit v1 on v0

v1 whole, which is shorter than its diff:
```python
import functools

import jax
import jax.numpy as jnp
from jax import lax
from jax.experimental import pallas as pl
from jax.experimental.pallas import tpu as pltpu
from jax.sharding import PartitionSpec as P

time_step = 0.15
VX, VY, VZ, SXX, SYY, SZZ, SXY, SXZ, SYZ = range(9)
MESH = pl.DeviceIdType.MESH


def kernel(
    gz_count,
    shot_count,
    wave_hbm,
    earth_hbm,
    src_depth_hbm,
    src_column_hbm,
    wavelet_hbm,
    rec_depth_hbm,
    rec_column_hbm,
    traces_hbm,
    out,
    state,
    earth,
    low0,
    high0,
    earth_low,
    earth_high,
    low,
    high,
    send_low,
    send_high,
    inject,
    press,
    image,
    parts_in,
    own,
    src_depth,
    src_column,
    wavelet,
    rec_depth,
    rec_column,
    traces,
    load_sem,
    init_send,
    init_recv,
    low_send,
    low_recv,
    high_send,
    high_recv,
    img_send,
    img_recv,
):
    planes, nx, ny = state.shape[2:]
    steps = traces.shape[0]
    h = time_step
    gz = lax.axis_index("gz")
    shot = lax.axis_index("shot")
    has_low = gz > 0
    has_high = gz < gz_count - 1

    load_wave = [
        pltpu.make_async_copy(wave_hbm.at[0, w], state.at[w], load_sem.at[w]) for w in range(2)
    ]
    load_earth = pltpu.make_async_copy(earth_hbm, earth, load_sem.at[2])
    small = [
        pltpu.make_async_copy(src, dst, load_sem.at[3 + i])
        for i, (src, dst) in enumerate(
            (
                (traces_hbm.at[0], traces),
                (rec_depth_hbm, rec_depth),
                (rec_column_hbm, rec_column),
                (src_depth_hbm, src_depth),
                (src_column_hbm, src_column),
                (wavelet_hbm, wavelet),
            )
        )
    ]
    for copy in small + [load_earth] + load_wave:
        copy.start()

    barrier = pltpu.get_barrier_semaphore()

    @pl.when(has_low)
    def _():
        pl.semaphore_signal(barrier, inc=1, device_id={"gz": gz - 1}, device_id_type=MESH)

    @pl.when(has_high)
    def _():
        pl.semaphore_signal(barrier, inc=1, device_id={"gz": gz + 1}, device_id_type=MESH)

    for k in range(1, shot_count):
        peer = lax.rem(shot + k, shot_count)
        pl.semaphore_signal(barrier, inc=1, device_id={"shot": peer}, device_id_type=MESH)

    low_peers = (gz + gz_count - 1) // gz_count
    high_peers = (2 * gz_count - 2 - gz) // gz_count
    pl.semaphore_wait(barrier, low_peers + high_peers + shot_count - 1)

    def remote(src, dst, sem, axis_to):
        return pltpu.make_async_remote_copy(
            src_ref=src,
            dst_ref=dst,
            send_sem=init_send.at[sem],
            recv_sem=init_recv.at[sem],
            device_id={"gz": axis_to},
            device_id_type=MESH,
        )

    last = planes - 1
    down = {
        w: [
            remote(wave_hbm.at[0, w, pl.ds(SXZ, 2), last], low0.at[w, pl.ds(2, 2)], 6 * w, gz + 1),
            remote(wave_hbm.at[0, w, SZZ, last], low0.at[w, 1], 6 * w + 1, gz + 1),
            remote(wave_hbm.at[0, w, VZ, last], low0.at[w, 0], 6 * w + 2, gz + 1),
        ]
        for w in range(2)
    }
    down_earth = remote(earth_hbm.at[0, last], earth_low, 12, gz + 1)
    up = {
        w: [
            remote(wave_hbm.at[0, w, pl.ds(SXX, 6), 0], high0.at[w, pl.ds(SXX, 6)], 6 * w + 3, gz - 1),
            remote(wave_hbm.at[0, w, pl.ds(VX, 2), 0], high0.at[w, pl.ds(VX, 2)], 6 * w + 4, gz - 1),
        ]
        for w in range(2)
    }
    up_earth = remote(earth_hbm.at[:, 0], earth_high, 13, gz - 1)
    down_all = down[0] + [down_earth] + down[1]
    up_all = up[0] + [up_earth] + up[1]

    @pl.when(has_high)
    def _():
        for copy in down_all:
            copy.start()

    @pl.when(has_low)
    def _():
        for copy in up_all:
            copy.start()

    @pl.when(jnp.logical_not(has_low))
    def _():
        low0[...] = jnp.zeros_like(low0)
        low[...] = jnp.zeros_like(low)
        earth_low[...] = jnp.zeros_like(earth_low)

    @pl.when(jnp.logical_not(has_high))
    def _():
        high0[...] = jnp.zeros_like(high0)
        high[...] = jnp.zeros_like(high)
        earth_high[...] = jnp.zeros_like(earth_high)

    image[...] = jnp.zeros_like(image)

    for copy in small:
        copy.wait()
    offset = gz * planes
    receivers = traces.shape[1]
    column = rec_column[...]
    depth = rec_depth[...] - offset
    row_ids = lax.broadcasted_iota(jnp.int32, (nx, receivers), 0) * ny
    past = column - row_ids
    on_row = (past >= 0) & (past < ny)
    row_hot = jnp.concatenate(
        [jnp.where(on_row & (depth == p), h, 0.0) for p in range(-1, planes)], axis=0
    )
    col_ids = lax.broadcasted_iota(jnp.int32, (ny, receivers), 0)
    col_hot = jnp.where((column & (ny - 1)) == col_ids, 1.0, 0.0)

    def fill(n, carry):
        inject[n] = lax.dot_general(
            row_hot * traces[pl.ds(n, 1), :],
            col_hot,
            (((1,), (1,)), ((), ())),
            precision=lax.Precision.HIGHEST,
            preferred_element_type=jnp.float32,
        ).reshape(planes + 1, nx, ny)
        return carry

    lax.fori_loop(0, steps, fill, 0)

    rows = lax.broadcasted_iota(jnp.int32, (nx, ny), 0)
    lanes = lax.broadcasted_iota(jnp.int32, (nx, ny), 1)
    cells = rows * ny + lanes

    def fx(a):
        return jnp.where(rows == nx - 1, 0.0, pltpu.roll(a, nx - 1, 0)) - a

    def bx(a):
        return a - jnp.where(rows == 0, 0.0, pltpu.roll(a, 1, 0))

    def fy(a):
        return jnp.where(lanes == ny - 1, 0.0, pltpu.roll(a, ny - 1, 1)) - a

    def by(a):
        return a - jnp.where(lanes == 0, 0.0, pltpu.roll(a, 1, 1))

    src_at = src_depth[0] - offset
    src_cell = src_column[0]

    def source_term(plane, n):
        cell = jnp.where(src_at == plane, src_cell, -1)
        return jnp.where(cells == cell, h * wavelet[0, n], 0.0)

    load_earth.wait()
    earth[...] = earth[...] * h

    def sends(w, n):
        to_high = pltpu.make_async_remote_copy(
            src_ref=send_low.at[w, n],
            dst_ref=low.at[w, n],
            send_sem=low_send.at[w, n],
            recv_sem=low_recv.at[w, n],
            device_id={"gz": gz + 1},
            device_id_type=MESH,
        )
        to_low = pltpu.make_async_remote_copy(
            src_ref=send_high.at[w, n],
            dst_ref=high.at[w, n],
            send_sem=high_send.at[w, n],
            recv_sem=high_recv.at[w, n],
            device_id={"gz": gz - 1},
            device_id_type=MESH,
        )
        return to_high, to_low

    def half(w, n, first, final):
        if first:
            load_wave[w].wait()

            @pl.when(has_low)
            def _():
                for copy in down[w]:
                    copy.wait_recv()
                if w == 0:
                    down_earth.wait_recv()

            @pl.when(has_high)
            def _():
                for copy in up[w]:
                    copy.wait_recv()
                if w == 0:
                    up_earth.wait_recv()

            szz_m, sxz_m, syz_m = (low0[w, i] for i in (1, 2, 3))
            sxz_p, syz_p = high0[w, SXZ], high0[w, SYZ]
        else:
            to_high, to_low = sends(w, n - 1)

            @pl.when(has_high)
            def _():
                to_low.wait_recv()

            @pl.when(has_low)
            def _():
                to_high.wait_recv()

            szz_m, sxz_m, syz_m = (low[w, n - 1, i] for i in range(3))
            vz_p, sxz_p, syz_p = (high[w, n - 1, i] for i in range(3))
            hlam = h * earth_high[1]
            hmu = h * earth_high[2]
            vx_p, vy_p = high0[w, VX], high0[w, VY]
            ex, ey, ez = bx(vx_p), by(vy_p), vz_p - state[w, VZ, last]
            spread = hlam * (ex + ey + ez)
            if w == 0:
                spread = spread + source_term(planes, n - 1)
            high0[w, SXX] += spread + 2.0 * hmu * ex
            high0[w, SYY] += spread + 2.0 * hmu * ey
            high0[w, SZZ] += spread + 2.0 * hmu * ez
            high0[w, SXY] += hmu * (fy(vx_p) + fx(vy_p))

        term = h * earth_low[...] * (bx(sxz_m) + by(syz_m) + (state[w, SZZ, 0] - szz_m))
        if w == 1:
            term = term + inject[n, 0]
        low0[w, 0] += term
        for p in range(planes):
            hb = earth[0, p]
            sxz, syz, szz, sxy = (state[w, i, p] for i in (SXZ, SYZ, SZZ, SXY))
            sxz_b = sxz_m if p == 0 else state[w, SXZ, p - 1]
            syz_b = syz_m if p == 0 else state[w, SYZ, p - 1]
            szz_f = high0[w, SZZ] if p == last else state[w, SZZ, p + 1]
            state[w, VX, p] += hb * (fx(state[w, SXX, p]) + by(sxy) + (sxz - sxz_b))
            state[w, VY, p] += hb * (bx(sxy) + fy(state[w, SYY, p]) + (syz - syz_b))
            term = hb * (bx(sxz) + by(syz) + (szz_f - szz))
            if w == 1:
                term = term + inject[n, p + 1]
            state[w, VZ, p] += term
        hb = h * earth_high[0]
        sxy = high0[w, SXY]
        high0[w, VX] += hb * (fx(high0[w, SXX]) + by(sxy) + (sxz_p - state[w, SXZ, last]))
        high0[w, VY] += hb * (bx(sxy) + fy(high0[w, SYY]) + (syz_p - state[w, SYZ, last]))

        def stress(p):
            vx, vy, vz = (state[w, i, p] for i in (VX, VY, VZ))
            vz_b = low0[w, 0] if p == 0 else state[w, VZ, p - 1]
            hmu = earth[2, p]
            ex, ey, ez = bx(vx), by(vy), vz - vz_b
            spread = earth[1, p] * (ex + ey + ez)
            if w == 0:
                spread = spread + source_term(p, n)
            mu2 = 2.0 * hmu
            sxx = state[w, SXX, p] + (spread + mu2 * ex)
            syy = state[w, SYY, p] + (spread + mu2 * ey)
            szz = state[w, SZZ, p] + (spread + mu2 * ez)
            pressure = (sxx + syy + szz) * (1.0 / 3.0)
            if not final:
                state[w, SXX, p] = sxx
                state[w, SYY, p] = syy
                state[w, SZZ, p] = szz
            if w == 1 or not final:
                vx_f = high0[w, VX] if p == last else state[w, VX, p + 1]
                vy_f = high0[w, VY] if p == last else state[w, VY, p + 1]
                vxz, vyz = vx_f - vx, vy_f - vy
                vzx, vzy, vxy, vyx = fx(vz), fy(vz), fy(vx), fx(vy)
            if not final:
                sxz = state[w, SXZ, p] + hmu * (vxz + vzx)
                syz = state[w, SYZ, p] + hmu * (vyz + vzy)
                state[w, SXY, p] += hmu * (vxy + vyx)
                state[w, SXZ, p] = sxz
                state[w, SYZ, p] = syz
                if p == 0:
                    send_high[w, n, 0] = vz
                    send_high[w, n, 1] = sxz
                    send_high[w, n, 2] = syz
                if p == last:
                    send_low[w, n, 0] = szz
                    send_low[w, n, 1] = sxz
                    send_low[w, n, 2] = syz
            if w == 0:
                press[p] = pressure
            else:
                rotation = (vzy - vyz) + (vxz - vzx) + (vyx - vxy)
                image[pl.ds(p * nx, nx), :] += press[p] * pressure
                image[pl.ds((planes + p) * nx, nx), :] += press[p] * rotation

        edge = sorted({0, last})
        for p in edge:
            stress(p)
        if not final:
            to_high, to_low = sends(w, n)

            @pl.when(has_low)
            def _():
                to_low.start()

            @pl.when(has_high)
            def _():
                to_high.start()

        for p in range(planes):
            if p not in edge:
                stress(p)

    def step(n, first, final):
        half(0, n, first, final)
        half(1, n, first, final)

    step(0, True, steps == 1)
    if steps > 2:

        def body(n, carry):
            step(n, False, False)
            return carry

        lax.fori_loop(1, steps - 1, body, 0)
    if steps > 1:
        step(steps - 1, False, True)

    total = image.shape[0]
    chunk = total // shot_count
    scale = 1.0 / steps

    def span(index):
        return pl.ds(pl.multiple_of(index * chunk, 8), chunk)

    scatter = []
    for k in range(1, shot_count):
        peer = lax.rem(shot + k, shot_count)
        copy = pltpu.make_async_remote_copy(
            src_ref=image.at[span(peer)],
            dst_ref=parts_in.at[k - 1],
            send_sem=img_send.at[0, k - 1],
            recv_sem=img_recv.at[0, k - 1],
            device_id={"shot": peer},
            device_id_type=MESH,
        )
        copy.start()
        scatter.append(copy)
    acc = image[span(shot), :]
    for k in range(1, shot_count):
        scatter[k - 1].wait_recv()
        acc = acc + parts_in[k - 1]
    acc = acc * scale
    own[...] = acc
    gather = []
    for k in range(1, shot_count):
        peer = lax.rem(shot + k, shot_count)
        copy = pltpu.make_async_remote_copy(
            src_ref=own,
            dst_ref=out.at[span(shot)],
            send_sem=img_send.at[1, k - 1],
            recv_sem=img_recv.at[1, k - 1],
            device_id={"shot": peer},
            device_id_type=MESH,
        )
        copy.start()
        gather.append(copy)
    out[span(shot), :] = acc

    @pl.when(has_high)
    def _():
        for copy in down_all:
            copy.wait_send()

    @pl.when(has_low)
    def _():
        for copy in up_all:
            copy.wait_send()

    def drain(n, carry):
        for w in range(2):
            to_high, to_low = sends(w, n)

            @pl.when(has_high)
            def _():
                to_high.wait_send()

            @pl.when(has_low)
            def _():
                to_low.wait_send()

        return carry

    lax.fori_loop(0, steps - 1, drain, 0)
    for copy in scatter:
        copy.wait_send()
    for copy in gather:
        copy.wait()


def on_device(
    gz_count,
    shot_count,
    wavefields,
    earth_model,
    source_depth,
    source_column,
    wavelet,
    receiver_depth,
    receiver_column,
    traces,
):
    planes, nx, ny = wavefields.shape[3:]
    steps = wavelet.shape[1]
    slots = max(steps - 1, 1)
    rows = 2 * planes * nx
    peers = max(shot_count - 1, 1)
    f32 = jnp.float32
    vmem = pl.BlockSpec(memory_space=pltpu.VMEM)
    hbm = pl.BlockSpec(memory_space=pl.ANY)
    dma = pltpu.SemaphoreType.DMA
    summed = pl.pallas_call(
        functools.partial(kernel, gz_count, shot_count),
        out_shape=jax.ShapeDtypeStruct((rows, ny), f32),
        in_specs=[hbm] * 8,
        out_specs=vmem,
        scratch_shapes=[
            pltpu.VMEM((2, 9, planes, nx, ny), f32),
            pltpu.VMEM((3, planes, nx, ny), f32),
            pltpu.VMEM((2, 4, nx, ny), f32),
            pltpu.VMEM((2, 9, nx, ny), f32),
            pltpu.VMEM((nx, ny), f32),
            pltpu.VMEM((3, nx, ny), f32),
            pltpu.VMEM((2, slots, 3, nx, ny), f32),
            pltpu.VMEM((2, slots, 3, nx, ny), f32),
            pltpu.VMEM((2, slots, 3, nx, ny), f32),
            pltpu.VMEM((2, slots, 3, nx, ny), f32),
            pltpu.VMEM((steps, planes + 1, nx, ny), f32),
            pltpu.VMEM((planes, nx, ny), f32),
            pltpu.VMEM((rows, ny), f32),
            pltpu.VMEM((peers, rows // shot_count, ny), f32),
            pltpu.VMEM((rows // shot_count, ny), f32),
            pltpu.SMEM(source_depth.shape, jnp.int32),
            pltpu.SMEM(source_column.shape, jnp.int32),
            pltpu.SMEM(wavelet.shape, f32),
            pltpu.VMEM(receiver_depth.shape, jnp.int32),
            pltpu.VMEM(receiver_column.shape, jnp.int32),
            pltpu.VMEM(traces.shape[1:], f32),
            dma((9,)),
            dma((14,)),
            dma((14,)),
            dma((2, slots)),
            dma((2, slots)),
            dma((2, slots)),
            dma((2, slots)),
            dma((2, peers)),
            dma((2, peers)),
        ],
        compiler_params=pltpu.CompilerParams(collective_id=0, has_side_effects=True),
    )(
        wavefields,
        earth_model,
        source_depth,
        source_column,
        wavelet,
        receiver_depth,
        receiver_column,
        traces,
    )
    return summed.reshape(2, planes, nx, ny)


def solution(mesh):
    placed = (
        P(("parts", "shot"), None, None, "gz", None, None),
        P("parts", "gz", None, None),
        P(("parts", "shot")),
        P(("parts", "shot")),
        P(("parts", "shot"), None),
        P(("parts", "shot"), None),
        P(("parts", "shot"), None),
        P(("parts", "shot"), None, None),
    )
    return jax.shard_map(
        functools.partial(on_device, mesh.shape["gz"], mesh.shape["shot"]),
        mesh=mesh,
        in_specs=placed,
        out_specs=P("parts", "gz", None, None),
        check_vma=False,
    )
```

time: 304 us -> 48.3 us (0.16)
  starting transfers between devices: 92.4 us -> 0 us
  other arithmetic: 77.9 us -> 0 us
  between operations: 67.3 us -> 1.3 us
  waiting for transfers between devices: 52.2 us -> 0 us
  Pallas kernels: 0 us -> 45.3 us
  local copies, waits for them, and re-layouts: 12.3 us -> 1.57 us
    ppermute x32 -> x0, starting transfers between devices: 92.4 us -> none  [shifted(): lax.ppermute(value, axis, [(source, source + steps) for source in range(f...]
    pallas_call x0 -> x1, Pallas kernels: none -> 45.3 us  [on_device(): pl.pallas_call(functools.partial(kernel, gz_count, shot_count), out_shape...]
    scatter-add x8 -> x0, other arithmetic: 42.2 us -> none  [add_points(): field_in.at[wave_index, place_at, row_index, col_index]]
    psum x1 -> x0, waiting for transfers between devices: 31.4 us -> none  [on_device(): lax.psum((tallies['image_pp'], tallies['image_ps']), 'shot')]
    add x63 -> x0, other arithmetic: 30 us -> none  [the longest x20 13 us: add_points(): field_in.at[wave_index, place_at, row_index, col_index]]
    ppermute x32 -> x0, waiting for transfers between devices: 20.9 us -> none  [shifted(): lax.ppermute(value, axis, [(source, source + steps) for source in range(f...]
    scatter-add x24 -> x0, local copies, waits for them, and re-layouts: 3.48 us -> none  [add_points(): field_in.at[wave_index, place_at, row_index, col_index]]
    slice x97 -> x0, local copies, waits for them, and re-layouts: 3.46 us -> none  [the longest x47 2.39 us: forward_diff(): lax.slice_in_dim(array, 1, length, axis=dim_index)]
  transfers between devices with their start and end apart: 33 -> 0, of which waited for: 11 -> 0; matrix products, arithmetic and copies ran while one was open for 19% -> 0% of each run, Pallas kernels for 0% -> 0%
where the time goes in v1:
time: 48.3 us; the launch traced here: 48.2 us
  Pallas kernels  45.3 us (94%)
  local copies, waits for them, and re-layouts  1.57 us (3%)
  between operations  1.3 us (3%)
    pallas_call x1, Pallas kernels, on_device(): pl.pallas_call(functools.partial(kernel, gz_count, shot_count), out_shape...  45.3 us
    unnamed x1, local copies, waits for them, and re-layouts  1.57 us

profile of v1, /device:TPU:0, one launch (start us, length us, event | category | flops | bytes accessed | tf_op | source)
XLA Modules:
  0.0 48.2 jit_solution(18376381054265762185)
XLA Ops:
  1.3 45.3 %shard_map.82 = f32[256,128]{1,0:T(8,128)} custom-call(f32[1,2,9,4,32,128]{5,4,3,2,1,0:T(8,128)} %wave_hbm.1, f32[3,4,32,128]{3,2,1,0:T(8,128)} %earth_hbm.1, s32[1]{0:T(128)S(6)} %copy.10.src_depth_hbm, s32[1]{0:T(128)S(6)} %copy.11.src_column_hbm, f32[1,8]{1,0:T(1,128)} %wavelet_hbm.1, s32[1,64]{1,0:T(1,128)} %rec_depth_hbm.1, s32[1,64]{1,0:T(1,128)} %rec_column_hbm.1, ...), custom_call_target="tpu_custom_call" | custom-call | tf_op jit(solution)/shard_map/pallas_call | solution.py:466
  46.6 1.6 %copy.12 = f32[2,4,32,128]{3,2,1,0:T(8,128)} copy(f32[2,4,32,128]{3,2,1,0:T(8,128)} %bitcast.1) | data formatting | bytes 262144

commit v2 on v1

--- a/solution.py
+++ b/solution.py
@@ -54,6 +54,7 @@
     high_recv,
     img_send,
     img_recv,
+    turn,
 ):
     planes, nx, ny = state.shape[2:]
     steps = traces.shape[0]
@@ -132,15 +133,23 @@
     down_all = down[0] + [down_earth] + down[1]
     up_all = up[0] + [up_earth] + up[1]
 
-    @pl.when(has_high)
-    def _():
-        for copy in down_all:
-            copy.start()
-
-    @pl.when(has_low)
-    def _():
-        for copy in up_all:
-            copy.start()
+    def start_first():
+        @pl.when(has_high)
+        def _():
+            for copy in down_all:
+                copy.start()
+
+        @pl.when(has_low)
+        def _():
+            for copy in up_all:
+                copy.start()
+
+    paired = shot_count % 2 == 0
+    even = lax.rem(shot, 2) == 0
+    if paired:
+        pl.when(even)(start_first)
+    else:
+        start_first()
 
     @pl.when(jnp.logical_not(has_low))
     def _():
@@ -182,6 +191,27 @@
         return carry
 
     lax.fori_loop(0, steps, fill, 0)
+
+    if paired:
+
+        @pl.when(even)
+        def _():
+            @pl.when(has_high)
+            def _():
+                for copy in down_all:
+                    copy.wait_send()
+
+            @pl.when(has_low)
+            def _():
+                for copy in up_all:
+                    copy.wait_send()
+
+            pl.semaphore_signal(turn, inc=1, device_id={"shot": shot + 1}, device_id_type=MESH)
+
+        @pl.when(jnp.logical_not(even))
+        def _():
+            pl.semaphore_wait(turn, 1)
+            start_first()
 
     rows = lax.broadcasted_iota(jnp.int32, (nx, ny), 0)
     lanes = lax.broadcasted_iota(jnp.int32, (nx, ny), 1)
@@ -411,12 +441,14 @@
         gather.append(copy)
     out[span(shot), :] = acc
 
-    @pl.when(has_high)
+    late = jnp.logical_not(even) if paired else shot >= 0
+
+    @pl.when(has_high & late)
     def _():
         for copy in down_all:
             copy.wait_send()
 
-    @pl.when(has_low)
+    @pl.when(has_low & late)
     def _():
         for copy in up_all:
             copy.wait_send()
@@ -499,6 +531,7 @@
             dma((2, slots)),
             dma((2, peers)),
             dma((2, peers)),
+            pltpu.SemaphoreType.REGULAR,
         ],
         compiler_params=pltpu.CompilerParams(collective_id=0, has_side_effects=True),
     )(

time: 48.3 us -> 46.5 us (0.963)
  Pallas kernels: 45.3 us -> 43.4 us
    pallas_call x1, Pallas kernels: 45.3 us -> 43.4 us  [on_device(): pl.pallas_call(functools.partial(kernel, gz_count, shot_count), out_shape...]
where the time goes in v2:
time: 46.5 us; the launch traced here: 46.3 us
  Pallas kernels  43.4 us (93%)
  local copies, waits for them, and re-layouts  1.57 us (3%)
  between operations  1.3 us (3%)
    pallas_call x1, Pallas kernels, on_device(): pl.pallas_call(functools.partial(kernel, gz_count, shot_count), out_shape...  43.4 us
    unnamed x1, local copies, waits for them, and re-layouts  1.57 us

profile of v2, /device:TPU:0, one launch (start us, length us, event | category | flops | bytes accessed | tf_op | source)
XLA Modules:
  0.0 46.3 jit_solution(18437812950495126130)
XLA Ops:
  1.3 43.4 %shard_map.82 = f32[256,128]{1,0:T(8,128)} custom-call(f32[1,2,9,4,32,128]{5,4,3,2,1,0:T(8,128)} %wave_hbm.1, f32[3,4,32,128]{3,2,1,0:T(8,128)} %earth_hbm.1, s32[1]{0:T(128)S(6)} %copy.10.src_depth_hbm, s32[1]{0:T(128)S(6)} %copy.11.src_column_hbm, f32[1,8]{1,0:T(1,128)} %wavelet_hbm.1, s32[1,64]{1,0:T(1,128)} %rec_depth_hbm.1, s32[1,64]{1,0:T(1,128)} %rec_column_hbm.1, ...), custom_call_target="tpu_custom_call" | custom-call | tf_op jit(solution)/shard_map/pallas_call | solution.py:498
  44.7 1.6 %copy.12 = f32[2,4,32,128]{3,2,1,0:T(8,128)} copy(f32[2,4,32,128]{3,2,1,0:T(8,128)} %bitcast.1) | data formatting | bytes 262144
